TPU v7x, 32 devices: a whole 2x2x4 slice. The times are simulated.
32 devices in a mesh: grp: 4 (over y, x), seq: 8 (over z, core).
Axes of the slice: x: 2, y: 2, z: 4, core: 2. Of those that a mesh axis runs over, the one named last changes fastest.
Arguments:
- tokens: bfloat16 [2048, 8192], P(None, 'seq'), may hold values from -16 to 16
- proj_weight: bfloat16 [8192, 5120], P('seq', 'grp'), may hold values from -0.0625 to 0.0625
- proj_bias: bfloat16 [5120], P('grp'), may hold values from -3 to 3
- out_weight: bfloat16 [4096, 8192], P('grp'), may hold values from -0.125 to 0.125
- doc_ids: int32 [2048], P('seq'), may hold values from 0 to 2, never falling along the last dimension, each value on 1 to 1280 neighbouring positions
Outputs:
- mixed: bfloat16 [2048, 8192], P('seq', 'grp')
Inputs may be any that keep to these rules, and one draw needn't show every extreme that they name: `doc_ids`: numbers never fall along the sequence; every document has 1 to 1280 tokens, one exactly that many; every number up to 2 is used.
All inputs are finite; a program needn't handle non-finite values.
Results may differ from a plain program's by a relative error of at most 0.012.
Values may be sent and summed in bfloat16 or wider, within the bound.
A program may use at most 256 MiB of HBM per device.

v0:
```python
import jax
import jax.numpy as jnp
from jax import lax
from jax.sharding import PartitionSpec as P

HEAD_DIM = 128
GQA = 8


theta_base = 1000000.0
neg_large = -1e30


def rotate(inputs, positions, head_dim):
    half_dim = head_dim // 2
    inverse_freq = theta_base ** (-(jnp.arange(half_dim, dtype=jnp.float32) * 2.0) / head_dim)
    angles = positions.astype(jnp.float32)[:, None] * inverse_freq[None, :]
    cosine = jnp.concatenate([jnp.cos(angles), jnp.cos(angles)], axis=1)
    sine_table = jnp.concatenate([jnp.sin(angles), jnp.sin(angles)], axis=1)
    low_half = inputs[..., :half_dim]
    high_half = inputs[..., half_dim:]
    turned = jnp.concatenate([-high_half, low_half], axis=-1)
    return inputs * cosine[:, None, :] + turned * sine_table[:, None, :]


def body(tokens, proj_weight, proj_bias, out_weight, doc_ids):
    tok_rows = doc_ids.shape[0]
    kv_local = proj_weight.shape[1] // ((GQA + 2) * HEAD_DIM)
    my_start = lax.axis_index("seq") * tok_rows
    projected = lax.psum_scatter(
        jnp.dot(tokens, proj_weight, preferred_element_type=jnp.float32),
        "seq",
        scatter_dimension=0,
        tiled=True,
    )
    projected = projected + proj_bias.astype(jnp.float32)[None, :]
    projected = projected.reshape(tok_rows, kv_local, GQA + 2, HEAD_DIM)
    positions = my_start + jnp.arange(tok_rows, dtype=jnp.int32)
    queries = rotate(
        projected[:, :, :GQA, :].reshape(tok_rows, kv_local * GQA, HEAD_DIM), positions, HEAD_DIM
    )
    queries = queries.astype(jnp.bfloat16).reshape(tok_rows, kv_local, GQA, HEAD_DIM)
    key_rows = rotate(projected[:, :, GQA, :], positions, HEAD_DIM).astype(jnp.bfloat16)
    value_rows = projected[:, :, GQA + 1, :].astype(jnp.bfloat16)
    score_scale = HEAD_DIM ** (-0.5)
    initial = (
        jnp.full((kv_local, GQA, tok_rows), neg_large, jnp.float32),
        jnp.zeros((kv_local, GQA, tok_rows), jnp.float32),
        jnp.zeros((kv_local, GQA, tok_rows, HEAD_DIM), jnp.float32),
    )
    key_block = lax.all_gather(key_rows, "seq", axis=0, tiled=True)
    value_block = lax.all_gather(value_rows, "seq", axis=0, tiled=True)
    block_ids = lax.all_gather(doc_ids, "seq", axis=0, tiled=True)
    key_index = jnp.arange(block_ids.shape[0], dtype=jnp.int32)
    allowed = (
        (block_ids[None, :] == doc_ids[:, None])
        & (key_index[None, :] <= positions[:, None])
        & (key_index[None, :] >= 0)
    )

    def compute(state):
        row_max, row_sum, weighted = state
        scores = (
            jnp.einsum("qkgd,pkd->kgqp", queries, key_block, preferred_element_type=jnp.float32)
            * score_scale
        )
        scores = jnp.where(allowed[None, None], scores, neg_large)
        new_max = jnp.maximum(row_max, jnp.max(scores, axis=-1))
        weights = jnp.where(allowed[None, None], jnp.exp(scores - new_max[..., None]), 0.0)
        new_sum = jnp.sum(weights, axis=-1)
        update = jnp.einsum(
            "kgqp,pkd->kgqd",
            weights.astype(jnp.bfloat16),
            value_block,
            preferred_element_type=jnp.float32,
        )
        return (new_max, new_sum, update)

    folded = lax.cond(jnp.any(allowed), compute, lambda state: state, initial)
    row_max, row_sum, weighted = folded
    outputs = (weighted / row_sum[..., None]).astype(jnp.bfloat16)
    attended = jnp.transpose(outputs, (2, 0, 1, 3)).reshape(tok_rows, kv_local * GQA * HEAD_DIM)
    partial_value = jnp.dot(attended, out_weight, preferred_element_type=jnp.float32)
    return lax.psum_scatter(partial_value, "grp", scatter_dimension=1, tiled=True).astype(
        jnp.bfloat16
    )


def solution(mesh):
    return jax.shard_map(
        body,
        mesh=mesh,
        in_specs=(P(None, "seq"), P("seq", "grp"), P("grp"), P("grp", None), P("seq")),
        out_specs=P("seq", "grp"),
        check_vma=False,
    )
```

profile of v0, /device:TPU:25, one launch (start us, length us, event | category | flops | bytes accessed | tf_op | source)
XLA Modules:
  0.0 281.7 jit_solution(13679033153051287310)
XLA Ops:
  6.5 0.0 copy-start
  6.5 0.0 reduce-scatter.3.cloned.1.call-start
  6.5 1.7 copy-done
  8.3 9.7 %fusion.27 = f32[2048,1280]{1,0:T(8,128)} fusion(bf16[2048,1024]{1,0:T(8,128)(2,1)} %param.7, bf16[1024,1280]{1,0:T(8,128)(2,1)S(1)} %copy-done), kind=kOutput, calls=%fused_computation.45 | convolution fusion | flops 5368709120 | bytes 17301504 | tf_op jit(solution)/shard_map/dot_general | solution.py:31
  18.0 0.0 copy-start.3
  18.0 0.0 copy-start.2
  18.0 0.0 reduce-scatter.3.cloned.1.call-update
  18.0 0.0 reduce-scatter.5.cloned.1.call-start
  18.0 0.6 copy-done.3
  18.6 0.0 copy-done.2
  18.6 8.2 %all-gather.1 = s32[8,1,256]{2,1,0:T(1,128)S(1)} all-gather(s32[1,1,256]{2,1,0:T(1,128)S(1)} %bitcast.80), channel_id=1, replica_groups=mesh['grp'=4,'seq'=8] {'seq'}, dimensions={0}, use_global_device_ids=true | all-gather | bytes 9216 | tf_op jit(solution)/shard_map/all_gather | solution.py:53
  26.8 1.2 fusion.17
  28.7 0.3 multiply_cosine_fusion
  29.1 96.7 %reduce-scatter.3.cloned.1.call-done = f32[256,1280]{1,0:T(8,128)} async-done(((f32[2048,1280]{1,0:T(8,128)}), f32[256,1280]{1,0:T(8,128)}) %reduce-scatter.3.cloned.1.call-update) | async-done | bytes 1310736 | tf_op jit(solution)/shard_map/reduce_scatter | solution.py:30
  125.7 2.5 broadcast_add_fusion
  128.2 1.7 copy.17
  130.0 0.1 slice_bitcast_fusion
  130.1 15.6 %all_gather.10 = bf16[2048,1,128]{0,2,1:T(8,128)(2,1)S(1)} all-gather(bf16[256,1,128]{0,2,1:T(8,128)(2,1)S(1)} %fusion.22), channel_id=1, replica_groups=mesh['grp'=4,'seq'=8] {'seq'}, dimensions={0}, use_global_device_ids=true | all-gather | bytes 589824 | tf_op jit(solution)/shard_map/all_gather | solution.py:51
  145.7 14.8 %all-gather = bf16[2048,1,1,128]{0,3,2,1:T(8,128)(2,1)S(1)} all-gather(bf16[256,1,1,128]{0,3,2,1:T(8,128)(2,1)S(1)} %slice.47), channel_id=2, replica_groups=mesh['grp'=4,'seq'=8] {'seq'}, dimensions={0}, use_global_device_ids=true | all-gather | bytes 589824 | tf_op jit(solution)/shard_map/all_gather | solution.py:52
  160.5 0.1 fusion.20
  160.6 0.2 fusion.19
  160.8 11.5 %conditional.1 = (f32[1,8,256]{2,1,0:T(8,128)S(1)}, f32[1,8,256,128]{2,3,1,0:T(8,128)S(1)}) conditional(s32[]{:T(128)} %convert_element_type.50, () %tuple.13, (pred[256,2048]{0,1:T(8,128)(4,1)S(1)}, bf16[2048,1,128]{0,2,1:T(8,128)(2,1)S(1)}, bf16[256,1,8,128]{0,3,2,1:T(8,128)(2,1)S(1)}, bf16[2048,1,128]{0,2,1:T(8,128)(2,1)S(1)}) %tuple.33), branch_computations={%region_2.0_spmd, %region_3.6_spmd} | conditional | flops 2202007552 | bytes 54575120 | solution.py:79
  160.8 2.8 fusion
  163.6 4.0 %fusion.2 = f32[8,256]{1,0:T(8,128)S(1)} fusion(f32[2048,256,8]{1,0,2:T(8,128)S(1)} %get-tuple-element.31, f32[8,256]{1,0:T(8,128)S(1)} %broadcast_maximum_fusion, pred[256,2048]{0,1:T(8,128)(4,1)S(1)} %get-tuple-element.13), kind=kLoop, calls=%fused_computation.4 | loop fusion | flops 20969472 | bytes 17317888 | tf_op jit(solution)/shard_map/cond/branch_1_fun/reduce_sum | solution.py:70
  167.7 4.5 %fusion.7 = f32[1,8,256,128]{2,3,1,0:T(8,128)S(1)} fusion(f32[2048,256,8]{1,0,2:T(8,128)S(1)} %get-tuple-element.31, f32[8,256]{1,0:T(8,128)S(1)} %broadcast_maximum_fusion, pred[256,2048]{0,1:T(8,128)(4,1)S(1)} %get-tuple-element.13, bf16[2048,1,128]{0,2,1:T(8,128)(2,1)S(1)} %get-tuple-element.28), kind=kOutput, calls=%fused_computation.8 | convolution fusion | flops 1094713344 | bytes 18882560 | tf_op jit(solution)/shard_map/cond/branch_1_fun/kgqp,pkd->kgqd/dot_general | solution.py:71
  172.3 0.1 divide_convert_fusion
  172.5 0.0 copy-start.1
  172.5 12.9 %fusion.28 = f32[256,8192]{1,0:T(8,128)} fusion(bf16[256,1024]{0,1:T(8,128)(2,1)S(1)} %bitcast.75, bf16[1024,8192]{1,0:T(8,128)(2,1)} %param.10), kind=kOutput, calls=%fused_computation.46 | convolution fusion | flops 4294967296 | bytes 25690112 | tf_op jit(solution)/shard_map/dot_general | solution.py:83
  185.3 0.0 reduce-scatter.5.cloned.1.call-update
  185.4 86.8 %reduce-scatter.5.cloned.1.call-done = f32[256,2048]{1,0:T(8,128)} async-done(((f32[256,8192]{1,0:T(8,128)}), f32[256,2048]{1,0:T(8,128)}) %reduce-scatter.5.cloned.1.call-update) | async-done | bytes 2097168 | tf_op jit(solution)/shard_map/reduce_scatter | solution.py:84
  272.2 2.7 convert_element_type.57
  274.9 0.0 copy-done.1
  (10 shorter events, 0.1 us)
Async XLA Ops:
  6.5 1.7 copy-start
  6.5 119.2 %reduce-scatter.3.cloned.1.call-start = ((), (), s32[]{:S(2)}) async-start(), calls=%async_computation.2 | async-start | bytes 11796480 | tf_op jit(solution)/shard_map/reduce_scatter | solution.py:30
  18.0 0.7 copy-start.3
  18.0 0.7 copy-start.2
  18.0 254.2 %reduce-scatter.5.cloned.1.call-start = ((), (), s32[]{:S(2)}) async-start(), calls=%async_computation.3 | async-start | bytes 10485760 | tf_op jit(solution)/shard_map/reduce_scatter | solution.py:84
  172.5 102.4 %copy-start.1 = (bf16[1024,1280]{1,0:T(8,128)(2,1)S(1)}, bf16[1024,1280]{1,0:T(8,128)(2,1)}, u32[]{:S(2)}) copy-start(bf16[1024,1280]{1,0:T(8,128)(2,1)} %param.8) | copy-start | bytes 7864324
Sparse Core Ops, SparseCore 0:
  18.1 107.5 reduce-scatter.2
  185.5 86.6 reduce-scatter.4
where the time goes:
time: 284 us; the launch traced here: 282 us
  waiting for transfers between devices  184 us (65%)
  blocking collectives  38.6 us (14%)
  matrix products  29.8 us (10%)
  between operations  14.2 us (5%)
  other arithmetic  11.2 us (4%)
  local copies, waits for them, and re-layouts  4.16 us (1%)
    reduce_scatter x1, waiting for transfers between devices, body(): lax.psum_scatter(jnp.dot(tokens, proj_weight, preferred_element_type=jnp....  96.7 us
    reduce_scatter x1, waiting for transfers between devices, body(): lax.psum_scatter(partial_value, 'grp', scatter_dimension=1, tiled=True)  86.8 us
    all_gather x1, blocking collectives, body(): key_block = lax.all_gather(key_rows, 'seq', axis=0, tiled=True)  15.6 us
    all_gather x1, blocking collectives, body(): value_block = lax.all_gather(value_rows, 'seq', axis=0, tiled=True)  14.8 us
    dot_general x1, matrix products, body(): jnp.dot(attended, out_weight, preferred_element_type=jnp.float32)  12.9 us
    dot_general x1, matrix products, body(): jnp.dot(tokens, proj_weight, preferred_element_type=jnp.float32)  9.68 us
    all_gather x1, blocking collectives, body(): block_ids = lax.all_gather(doc_ids, 'seq', axis=0, tiled=True)  8.16 us
  transfers between devices with their start and end apart: 2, of which 2 were waited for; matrix products, arithmetic and copies ran while one was open for 1% of the time, Pallas kernels for 0%

commit v1 on v0

v1 whole, which is shorter than its diff:
```python
import functools

import jax
import jax.numpy as jnp
from jax import lax
from jax.experimental import pallas as pl
from jax.experimental.pallas import tpu as pltpu
from jax.sharding import PartitionSpec as P

HEAD_DIM = 128
GQA = 8
MESH = pl.DeviceIdType.MESH

theta_base = 1000000.0
neg_large = -1e30


def rope_tables(positions, head_dim):
    half_dim = head_dim // 2
    inverse_freq = theta_base ** (-(jnp.arange(half_dim, dtype=jnp.float32) * 2.0) / head_dim)
    angles = positions.astype(jnp.float32)[:, None] * inverse_freq[None, :]
    cosine, sine = jnp.cos(angles), jnp.sin(angles)
    return jnp.concatenate([cosine, cosine], axis=1), jnp.concatenate([-sine, sine], axis=1)


def proj_kernel(
    line, chunks, rows, width,
    tok_ref, w_ref, bias_ref, cos_ref, sin_ref, ids_ref,
    q_ref, kv_ref, idall_ref,
    pair_out, pair_in, up_in, dn_in, total,
    pair_ss, pair_rs, line_ss, up_rs, dn_rs, id_ss, id_rs, kvl_ss, kvl_rs, kvp_ss, kvp_rs,
):
    g = lax.axis_index("grp")
    s = lax.axis_index("seq")
    z, c = s // 2, lax.rem(s, 2)
    n = 2 * line
    partner = s + 1 - 2 * c
    low = z < line // 2

    barrier = pltpu.get_barrier_semaphore()
    for i in range(1, n):
        pl.semaphore_signal(barrier, inc=1, device_id=(g, lax.rem(s + i, n)), device_id_type=MESH)
    pl.semaphore_wait(barrier, n - 1)

    def id_copy(i):
        return pltpu.make_async_remote_copy(
            ids_ref, idall_ref.at[s], id_ss.at[i], id_rs.at[i],
            device_id=(g, lax.rem(s + i, n)), device_id_type=MESH,
        )

    def id_wait(i):
        return pltpu.make_async_remote_copy(
            ids_ref, idall_ref.at[lax.rem(s + n - i, n)], id_ss.at[i], id_rs.at[i],
            device_id=(g, lax.rem(s + i, n)), device_id_type=MESH,
        )

    idall_ref[s] = ids_ref[...]

    def offset(kk):
        return pl.multiple_of(lax.rem(kk + chunks - 1, chunks) * width, width)

    def product(kk, dest, core):
        row = pl.multiple_of((2 * dest + core) * rows, rows)
        return jnp.dot(
            tok_ref[pl.ds(row, rows), :], w_ref[:, pl.ds(offset(kk), width)],
            preferred_element_type=jnp.float32,
        )

    def pair_copy(kk, dest):
        return pltpu.make_async_remote_copy(
            pair_out.at[kk, dest], pair_in.at[kk, dest], pair_ss.at[kk, dest], pair_rs.at[kk, dest],
            device_id=(g, partner), device_id_type=MESH,
        )

    def up_copy(kk, dest):
        return pltpu.make_async_remote_copy(
            pair_in.at[kk, dest], up_in.at[kk, dest], line_ss.at[kk, dest], up_rs.at[kk, dest],
            device_id=(g, lax.rem(s + 2, n)), device_id_type=MESH,
        )

    def dn_copy(kk, dest):
        return pltpu.make_async_remote_copy(
            pair_in.at[kk, dest], dn_in.at[kk, dest], line_ss.at[kk, dest], dn_rs.at[kk, dest],
            device_id=(g, lax.rem(s + n - 2, n)), device_id_type=MESH,
        )

    def kv_line(zz):
        block = kv_ref.at[2 * zz + c]
        return pltpu.make_async_remote_copy(
            block, block, kvl_ss.at[zz], kvl_rs.at[zz], device_id=(g, lax.rem(s + 2, n)), device_id_type=MESH
        )

    def kv_pair(zz):
        block = kv_ref.at[2 * zz + c]
        return pltpu.make_async_remote_copy(
            block, block, kvp_ss.at[zz], kvp_rs.at[zz], device_id=(g, partner), device_id_type=MESH
        )

    def kv_pair_wait(zz):
        block = kv_ref.at[2 * zz + 1 - c]
        return pltpu.make_async_remote_copy(
            block, block, kvp_ss.at[zz], kvp_rs.at[zz], device_id=(g, partner), device_id_type=MESH
        )

    def pair_stage(kk):
        @pl.loop(0, line)
        def _(i):
            dest = jnp.where(low, line - 1 - i, i)
            pair_out[kk, dest] = product(kk, dest, 1 - c).astype(jnp.bfloat16)
            pair_copy(kk, dest).start()

    def gathered(kk, dest):
        total[...] = product(kk, dest, c)
        pair_copy(kk, dest).wait_recv()
        total[...] += pair_in[kk, dest].astype(jnp.float32)

    def up_stage(kk):
        @pl.loop(0, line - 1 - z)
        def _(d):
            dest = line - 1 - d
            gathered(kk, dest)

            @pl.when(z > 0)
            def _():
                up_copy(kk, dest).wait_recv()
                total[...] += up_in[kk, dest].astype(jnp.float32)

            pair_in[kk, dest] = total[...].astype(jnp.bfloat16)
            up_copy(kk, dest).start()

    def dn_stage(kk):
        @pl.loop(0, z)
        def _(dest):
            gathered(kk, dest)

            @pl.when(z < line - 1)
            def _():
                dn_copy(kk, dest).wait_recv()
                total[...] += dn_in[kk, dest].astype(jnp.float32)

            pair_in[kk, dest] = total[...].astype(jnp.bfloat16)
            dn_copy(kk, dest).start()

    def wait_up_sends(kk):
        @pl.loop(0, line - 1 - z)
        def _(d):
            up_copy(kk, line - 1 - d).wait_send()

    def wait_dn_sends(kk):
        @pl.loop(0, z)
        def _(dest):
            dn_copy(kk, dest).wait_send()

    def rope(x):
        return x * cos_ref[...] + pltpu.roll(x, HEAD_DIM // 2, 1) * sin_ref[...]

    def finish(kk):
        gathered(kk, z)

        @pl.when(z > 0)
        def _():
            up_copy(kk, z).wait_recv()
            total[...] += up_in[kk, z].astype(jnp.float32)

        @pl.when(z < line - 1)
        def _():
            dn_copy(kk, z).wait_recv()
            total[...] += dn_in[kk, z].astype(jnp.float32)

        total[...] += bias_ref[:, pl.ds(offset(kk), width)]

        @pl.when(kk == 0)
        def _():
            kv_ref[s, :, :HEAD_DIM] = rope(total[:, :HEAD_DIM]).astype(jnp.bfloat16)
            kv_ref[s, :, HEAD_DIM:] = total[:, HEAD_DIM:].astype(jnp.bfloat16)
            kv_pair(z).start()

            @pl.when(z < line - 1)
            def _():
                kv_line(z).start()

        @pl.when(kk > 0)
        def _():
            for half in range(width // HEAD_DIM):
                lanes = slice(half * HEAD_DIM, (half + 1) * HEAD_DIM)
                q_ref[:, pl.ds(offset(kk) + half * HEAD_DIM, HEAD_DIM)] = rope(total[:, lanes]).astype(jnp.bfloat16)

    def relay(h):
        @pl.when(h <= z)
        def _():
            zz = z - h
            kv_line(zz).wait_recv()

            @pl.when(z < line - 1)
            def _():
                kv_line(zz).start()

            kv_pair(zz).start()

    pair_stage(0)
    for i in range(1, n):
        id_copy(i).start()

    @pl.loop(0, chunks + 2)
    def _(kk):
        @pl.when(kk >= 2)
        def _():
            @pl.when(low)
            def _():
                wait_up_sends(kk - 2)

            @pl.when(jnp.logical_not(low))
            def _():
                wait_dn_sends(kk - 2)

        @pl.when(kk < chunks)
        def _():
            @pl.when(low)
            def _():
                up_stage(kk)

            @pl.when(jnp.logical_not(low))
            def _():
                dn_stage(kk)

        @pl.when(kk + 1 < chunks)
        def _():
            pair_stage(kk + 1)

        @pl.when((kk >= 1) & (kk <= chunks))
        def _():
            @pl.when(low)
            def _():
                dn_stage(kk - 1)

            @pl.when(jnp.logical_not(low))
            def _():
                up_stage(kk - 1)

        @pl.when(kk >= 2)
        def _():
            finish(kk - 2)

        @pl.when(kk >= 4)
        def _():
            relay(kk - 3)

    @pl.loop(chunks - 1, line)
    def _(h):
        relay(h)

    @pl.loop(0, chunks)
    def _(kk):
        @pl.when(low)
        def _():
            wait_dn_sends(kk)

        @pl.when(jnp.logical_not(low))
        def _():
            wait_up_sends(kk)

        @pl.loop(0, line)
        def _(dest):
            pair_copy(kk, dest).wait_send()

    @pl.loop(0, z + 1)
    def _(zz):
        kv_pair_wait(zz).wait_recv()
        kv_pair(zz).wait_send()

        @pl.when(z < line - 1)
        def _():
            kv_line(zz).wait_send()

    for i in range(1, n):
        id_copy(i).wait_send()
        id_wait(i).wait_recv()


def attention_kernel(blocks, rows, place_ref, q_ref, kv_ref, idall_ref, idcol_ref, out_ref):
    first, last = place_ref[0], place_ref[1]
    scale = HEAD_DIM ** (-0.5)
    row_ids = idcol_ref[:, :1]
    ahead = lax.broadcasted_iota(jnp.int32, (rows, rows), 1) - lax.broadcasted_iota(jnp.int32, (rows, rows), 0)
    ones = jnp.ones((rows, HEAD_DIM), jnp.bfloat16)

    @pl.loop(0, GQA // 2)
    def _(pair):
        lanes = [pl.multiple_of((2 * pair + i) * HEAD_DIM, HEAD_DIM) for i in range(2)]
        queries = [q_ref[:, pl.ds(lane, HEAD_DIM)] for lane in lanes]

        def step(j, state):
            keys = kv_ref[j, :, :HEAD_DIM]
            values = jnp.concatenate([kv_ref[j, :, HEAD_DIM:], ones], axis=1)
            allowed = (row_ids == idall_ref[j, :1, :]) & (ahead <= (last - j) * rows)
            new = []
            for i in range(2):
                row_max, weighted = state[i]
                scores = lax.dot_general(
                    queries[i], keys, (((1,), (1,)), ((), ())), preferred_element_type=jnp.float32
                )
                scores = jnp.where(allowed, scores * scale, neg_large)
                new_max = jnp.maximum(row_max, jnp.max(scores, axis=1, keepdims=True))
                weights = jnp.where(allowed, jnp.exp(scores - new_max), 0.0)
                update = jnp.dot(weights.astype(jnp.bfloat16), values, preferred_element_type=jnp.float32)
                new.append((new_max, weighted * jnp.exp(row_max - new_max) + update))
            return tuple(new)

        initial = (
            jnp.full((rows, 1), neg_large, jnp.float32),
            jnp.zeros((rows, 2 * HEAD_DIM), jnp.float32),
        )
        state = lax.fori_loop(first, last + 1, step, (initial, initial))
        for i in range(2):
            weighted = state[i][1]
            out_ref[:, pl.ds(lanes[i], HEAD_DIM)] = (weighted[:, :HEAD_DIM] / weighted[:, HEAD_DIM:]).astype(
                jnp.bfloat16
            )


def out_kernel(
    groups, tiles, rows, width,
    att_ref, w_ref, out_ref,
    weights, kept, passing_x, passing_y, send1, recv1, send2, recv2,
    w_sem, ss1, rs1, ss2, rs2,
):
    g = lax.axis_index("grp")
    s = lax.axis_index("seq")
    peer_x = g + 1 - 2 * lax.rem(g, 2)
    peer_y = lax.rem(g + 2, groups)
    diagonal = groups - 1 - g
    peers = (peer_x, peer_y)
    half = rows // 2
    order = (diagonal, peer_x, peer_y, g)

    def w_copy(i, t):
        column = pl.multiple_of((order[i] * tiles + t) * width, width)
        return pltpu.make_async_copy(w_ref.at[:, pl.ds(column, width)], weights.at[i, t], w_sem.at[i, t])

    for i in range(4):
        @pl.loop(0, tiles)
        def _(t):
            w_copy(i, t).start()

    barrier = pltpu.get_barrier_semaphore()
    for peer in peers:
        pl.semaphore_signal(barrier, inc=1, device_id=(peer, s), device_id_type=MESH)
    pl.semaphore_wait(barrier, 2)

    def copy1(way, slot, t):
        return pltpu.make_async_remote_copy(
            send1.at[way, slot, t], recv1.at[way, slot, t], ss1.at[way, slot, t], rs1.at[way, slot, t],
            device_id=(peers[way], s), device_id_type=MESH,
        )

    def copy2(way, t):
        return pltpu.make_async_remote_copy(
            send2.at[way, t], recv2.at[way, t], ss2.at[way, t], rs2.at[way, t],
            device_id=(peers[way], s), device_id_type=MESH,
        )

    def product(i, t):
        w_copy(i, t).wait()
        return jnp.dot(att_ref[...], weights[i, t], preferred_element_type=jnp.float32)

    @pl.loop(0, tiles)
    def _(t):
        value = product(0, t).astype(jnp.bfloat16)
        send1[0, 0, t] = value[:half]
        send1[1, 0, t] = value[half:]
        copy1(0, 0, t).start()
        copy1(1, 0, t).start()

    @pl.loop(0, tiles)
    def _(t):
        value = product(1, t)
        send1[0, 1, t] = value[:half].astype(jnp.bfloat16)
        copy1(0, 1, t).start()
        passing_x[t] = value[half:]
        value = product(2, t)
        send1[1, 1, t] = value[half:].astype(jnp.bfloat16)
        copy1(1, 1, t).start()
        passing_y[t] = value[:half]

    @pl.loop(0, tiles)
    def _(t):
        copy1(1, 0, t).wait_recv()
        send2[0, t] = (passing_x[t] + recv1[1, 0, t].astype(jnp.float32)).astype(jnp.bfloat16)
        copy2(0, t).start()
        copy1(0, 0, t).wait_recv()
        send2[1, t] = (passing_y[t] + recv1[0, 0, t].astype(jnp.float32)).astype(jnp.bfloat16)
        copy2(1, t).start()

    @pl.loop(0, tiles)
    def _(t):
        kept[t] = product(3, t)

    for t in range(tiles):
        copy1(0, 1, t).wait_recv()
        copy1(1, 1, t).wait_recv()
        copy2(0, t).wait_recv()
        copy2(1, t).wait_recv()
        lanes = slice(t * width, (t + 1) * width)
        out_ref[:half, lanes] = (
            kept[t, :half] + recv1[0, 1, t].astype(jnp.float32) + recv2[1, t].astype(jnp.float32)
        ).astype(jnp.bfloat16)
        out_ref[half:, lanes] = (
            kept[t, half:] + recv1[1, 1, t].astype(jnp.float32) + recv2[0, t].astype(jnp.float32)
        ).astype(jnp.bfloat16)

    @pl.loop(0, tiles)
    def _(t):
        for way in range(2):
            copy1(way, 0, t).wait_send()
            copy1(way, 1, t).wait_send()
            copy2(way, t).wait_send()


def body(seq, groups, tokens, proj_weight, proj_bias, out_weight, doc_ids):
    rows = doc_ids.shape[0]
    columns = proj_weight.shape[1]
    width = 2 * HEAD_DIM
    chunks = columns // width
    line = seq // 2
    q_width = GQA * HEAD_DIM
    start = lax.axis_index("seq") * rows
    positions = start + jnp.arange(rows, dtype=jnp.int32)
    cosine, sine = rope_tables(positions, HEAD_DIM)
    vmem = pl.BlockSpec(memory_space=pltpu.VMEM)
    dma = pltpu.SemaphoreType.DMA
    bf16, f32 = jnp.bfloat16, jnp.float32
    limit = 62 * 1024 * 1024

    queries, kv, id_blocks = pl.pallas_call(
        functools.partial(proj_kernel, line, chunks, rows, width),
        out_shape=(
            jax.ShapeDtypeStruct((rows, q_width), bf16),
            jax.ShapeDtypeStruct((seq, rows, width), bf16),
            jax.ShapeDtypeStruct((seq, 8, rows), jnp.int32),
        ),
        in_specs=[vmem] * 6,
        out_specs=(vmem, vmem, vmem),
        scratch_shapes=[pltpu.VMEM((chunks, line, rows, width), bf16)] * 4
        + [pltpu.VMEM((rows, width), f32)]
        + [dma((chunks, line))] * 5
        + [dma((seq,))] * 2
        + [dma((line,))] * 4,
        compiler_params=pltpu.CompilerParams(collective_id=0, has_side_effects=True, vmem_limit_bytes=limit),
        name="proj_scatter",
    )(
        tokens,
        proj_weight,
        proj_bias.astype(f32)[None, :],
        cosine,
        sine,
        jnp.broadcast_to(doc_ids[None, :], (8, rows)),
    )

    place = jnp.stack(
        [jnp.sum((id_blocks[:, 0, rows - 1] < doc_ids[0]).astype(jnp.int32)), lax.axis_index("seq")]
    ).astype(jnp.int32)
    attended = pl.pallas_call(
        functools.partial(attention_kernel, seq, rows),
        out_shape=jax.ShapeDtypeStruct((rows, q_width), bf16),
        in_specs=[pl.BlockSpec(memory_space=pltpu.SMEM)] + [vmem] * 4,
        out_specs=vmem,
        compiler_params=pltpu.CompilerParams(vmem_limit_bytes=limit),
        name="attention",
    )(place, queries, kv, id_blocks, jnp.broadcast_to(doc_ids[:, None], (rows, HEAD_DIM)))

    block = out_weight.shape[1] // groups
    tile = 2 * width
    tiles = block // tile
    half = rows // 2
    return pl.pallas_call(
        functools.partial(out_kernel, groups, tiles, rows, tile),
        out_shape=jax.ShapeDtypeStruct((rows, block), bf16),
        in_specs=[vmem, pl.BlockSpec(memory_space=pl.ANY)],
        out_specs=vmem,
        scratch_shapes=[
            pltpu.VMEM((4, tiles, q_width, tile), bf16),
            pltpu.VMEM((tiles, rows, tile), f32),
            pltpu.VMEM((tiles, half, tile), f32),
            pltpu.VMEM((tiles, half, tile), f32),
            pltpu.VMEM((2, 2, tiles, half, tile), bf16),
            pltpu.VMEM((2, 2, tiles, half, tile), bf16),
            pltpu.VMEM((2, tiles, half, tile), bf16),
            pltpu.VMEM((2, tiles, half, tile), bf16),
            dma((4, tiles)),
            dma((2, 2, tiles)),
            dma((2, 2, tiles)),
            dma((2, tiles)),
            dma((2, tiles)),
        ],
        compiler_params=pltpu.CompilerParams(collective_id=1, has_side_effects=True, vmem_limit_bytes=limit),
        name="out_scatter",
    )(attended, out_weight)


def solution(mesh):
    return jax.shard_map(
        functools.partial(body, mesh.shape["seq"], mesh.shape["grp"]),
        mesh=mesh,
        in_specs=(P(None, "seq"), P("seq", "grp"), P("grp"), P("grp", None), P("seq")),
        out_specs=P("seq", "grp"),
        check_vma=False,
    )
```

time: 284 us -> 131 us (0.46); the launches traced: 282 us -> 133 us
  waiting for transfers between devices: 184 us -> 0 us
  Pallas kernels: 0 us -> 121 us
  blocking collectives: 38.6 us -> 0 us
  matrix products: 29.8 us -> 0 us
  between operations: 14.2 us -> 0.03 us
  other arithmetic: 11.2 us -> 4.7 us
  local copies, waits for them, and re-layouts: 4.16 us -> 7.49 us
    reduce_scatter x2 -> x0, waiting for transfers between devices: 183 us -> none  [the longest x1 96.7 us: body(): lax.psum_scatter(jnp.dot(tokens, proj_weight, preferred_element_type=jnp....]
    pallas_call x0 -> x3, Pallas kernels: none -> 121 us  [the longest x1 66.6 us: body(): pl.pallas_call(functools.partial(proj_kernel, line, chunks, rows, width),...]
    all_gather x3 -> x0, blocking collectives: 38.6 us -> none  [the longest x1 15.6 us: body(): key_block = lax.all_gather(key_rows, 'seq', axis=0, tiled=True)]
    dot_general x4 -> x0, matrix products: 29.8 us -> none  [the longest x1 12.9 us: body(): jnp.dot(attended, out_weight, preferred_element_type=jnp.float32)]
    broadcast_in_dim x0 -> x3, local copies, waits for them, and re-layouts: none -> 3.98 us  [the longest x1 1.43 us: body(): jnp.broadcast_to(doc_ids[:, None], (rows, HEAD_DIM))]
    convert_element_type x6 -> x1, other arithmetic: 3.06 us -> 0.01 us  [rope_tables(): angles = positions.astype(jnp.float32)[:, None] * inverse_freq[None, :]]
  transfers between devices with their start and end apart: 2 -> 0, of which waited for: 2 -> 0; matrix products, arithmetic and copies ran while one was open for 1% -> 0% of each run, Pallas kernels for 0% -> 0%
where the time goes in v1:
time: 131 us; the launch traced here: 133 us
  Pallas kernels  121 us (92%)
  local copies, waits for them, and re-layouts  7.49 us (6%)
  other arithmetic  4.7 us (4%)
    pallas_call x1, Pallas kernels, body(): pl.pallas_call(functools.partial(proj_kernel, line, chunks, rows, width),...  66.6 us
    pallas_call x1, Pallas kernels, body(): pl.pallas_call(functools.partial(out_kernel, groups, tiles, rows, tile),...  38.3 us
    pallas_call x1, Pallas kernels, body(): pl.pallas_call(functools.partial(attention_kernel, seq, rows), out_shape=...  15.6 us

profile of v1, /device:TPU:25, one launch (start us, length us, event | category | flops | bytes accessed | tf_op | source)
XLA Modules:
  0.0 132.8 jit_solution(15084910358370272280)
XLA Ops:
  0.0 1.2 slice.7
  1.2 1.3 reshape.17.bias_ref
  2.5 1.3 broadcast_in_dim.10.ids_ref
  3.8 1.4 %broadcast_in_dim.22.idcol_ref = s32[256,128]{1,0:T(8,128)} broadcast(s32[256]{0:T(256)} %param.9), dimensions={0} | broadcast | bytes 132096 | tf_op jit(solution)/shard_map/broadcast_in_dim | solution.py:469
  5.2 0.5 fusion
  5.7 0.8 pad_maximum_fusion
  6.6 66.6 %proj_scatter.1 = (bf16[256,1024]{1,0:T(8,128)(2,1)}, bf16[8,256,256]{2,1,0:T(8,128)(2,1)}, s32[8,8,256]{2,1,0:T(8,128)}) custom-call(bf16[2048,1024]{1,0:T(8,128)(2,1)} %tok_ref.1, bf16[1024,1280]{1,0:T(8,128)(2,1)} %w_ref.2, f32[1,1280]{1,0:T(1,128)} %reshape.17.bias_ref, f32[256,128]{1,0:T(8,128)} %get-tuple-element.14.cos_ref, ...), custom_call_target="tpu_custom_call" | custom-call | tf_op jit(solution)/shard_map/proj_scatter/pallas_call | solution.py:434
  73.2 2.1 %fusion.1 = s32[]{:T(128)} fusion(s32[8,8,256]{2,1,0:T(8,128)} %get-tuple-element.8.idall_ref, s32[]{:T(128)} %bitcast), kind=kLoop, calls=%fused_computation.6 | loop fusion | flops 23 | bytes 40 | tf_op jit(solution)/shard_map/reduce_sum | solution.py:460
  75.3 1.2 pad_add_fusion.place_ref
  76.5 15.6 %attention.1.att_ref = bf16[256,1024]{1,0:T(8,128)(2,1)} custom-call(s32[2]{0:T(128)} %pad_add_fusion.place_ref, bf16[256,1024]{1,0:T(8,128)(2,1)} %get-tuple-element.9.q_ref, bf16[8,256,256]{2,1,0:T(8,128)(2,1)} %get-tuple-element.10.kv_ref, s32[8,8,256]{2,1,0:T(8,128)} %get-tuple-element.8.idall_ref, s32[256,128]{1,0:T(8,128)} %broadcast_in_dim.22.idcol_ref), custom_call_target="tpu_custom_call" | custom-call | tf_op jit(solution)/shard_map/attention/pallas_call | solution.py:462
  92.1 38.3 %out_scatter.1 = bf16[256,2048]{1,0:T(8,128)(2,1)} custom-call(bf16[256,1024]{1,0:T(8,128)(2,1)} %attention.1.att_ref, bf16[1024,8192]{1,0:T(8,128)(2,1)} %w_ref.3), custom_call_target="tpu_custom_call" | custom-call | tf_op jit(solution)/shard_map/out_scatter/pallas_call | solution.py:475
  130.5 2.3 %copy.7 = bf16[256,2048]{1,0:T(8,128)(2,1)} copy(bf16[256,2048]{1,0:T(8,128)(2,1)} %out_scatter.1) | data formatting | bytes 2097152
  (2 shorter events, 0.0 us)

commit v2 on v0

v2 whole, which is shorter than its diff:
```python
import functools

import jax
import jax.numpy as jnp
from jax import lax
from jax.experimental import pallas as pl
from jax.experimental.pallas import tpu as pltpu
from jax.sharding import PartitionSpec as P

HEAD_DIM = 128
GQA = 8
MESH = pl.DeviceIdType.MESH

theta_base = 1000000.0
neg_large = -1e30


def layer_kernel(
    line, chunks, rows, width, groups, tiles, wide, slots,
    tok_ref, w_ref, bias_ref, freq_ref, ids_ref, ow_ref,
    out_ref,
    pair_out, pair_in, up_in, dn_in, total, queries, kv_ref, attended, ids_own, ids_col, idall_ref,
    bias, cos_ref, sin_ref, weights, kept, send1, recv1, send2, recv2,
    pair_ss, pair_rs, line_ss, up_rs, dn_rs, id_ss, id_rs, kvl_ss, kvl_rs, kvp_ss, kvp_rs,
    w_sem, ss1, rs1, ss2, rs2,
):
    g = lax.axis_index("grp")
    s = lax.axis_index("seq")
    z, c = s // 2, lax.rem(s, 2)
    n = 2 * line
    partner = s + 1 - 2 * c
    low = z < line // 2
    half = rows // 2
    peer_x = g + 1 - 2 * lax.rem(g, 2)
    peer_y = lax.rem(g + 2, groups)
    passes = 4 * tiles

    def first_peer(t):
        return jnp.where(lax.rem(t, 2) == 0, peer_x, peer_y)

    def second_peer(t):
        return jnp.where(lax.rem(t, 2) == 0, peer_y, peer_x)

    def w_copy(m):
        pos, t = lax.rem(m // tiles, 4), lax.rem(m, tiles)
        block = jnp.where(
            pos == 0, groups - 1 - g, jnp.where(pos == 1, first_peer(t), jnp.where(pos == 2, g, second_peer(t)))
        )
        column = pl.multiple_of((block * tiles + t) * wide, wide)
        slot = lax.rem(m, slots)
        return pltpu.make_async_copy(ow_ref.at[:, pl.ds(column, wide)], weights.at[slot], w_sem.at[slot])

    @pl.loop(0, slots)
    def _(m):
        w_copy(m).start()

    row_ids = jnp.broadcast_to(ids_ref[...].reshape(1, rows), (HEAD_DIM, rows))
    ids_own[...] = row_ids[:8]
    ids_col[...] = row_ids.T
    bias[...] = jnp.broadcast_to(bias_ref[...].astype(jnp.float32), bias.shape)

    barrier = pltpu.get_barrier_semaphore()
    for i in range(1, n):
        pl.semaphore_signal(barrier, inc=1, device_id=(g, lax.rem(s + i, n)), device_id_type=MESH)
    for peer in (peer_x, peer_y):
        pl.semaphore_signal(barrier, inc=1, device_id=(peer, s), device_id_type=MESH)
    pl.semaphore_wait(barrier, n + 1)

    def id_copy(i):
        return pltpu.make_async_remote_copy(
            ids_own, idall_ref.at[s], id_ss.at[i], id_rs.at[i],
            device_id=(g, lax.rem(s + i, n)), device_id_type=MESH,
        )

    def id_wait(i):
        return pltpu.make_async_remote_copy(
            ids_own, idall_ref.at[lax.rem(s + n - i, n)], id_ss.at[i], id_rs.at[i],
            device_id=(g, lax.rem(s + i, n)), device_id_type=MESH,
        )

    idall_ref[s] = ids_own[...]

    def product(kk, dest, core, put):
        row = (2 * dest + core) * rows

        @pl.when(kk == 0)
        def _():
            put(slice(None), jnp.dot(
                tok_ref[pl.ds(pl.multiple_of(row, rows), rows), :], w_ref[:, (chunks - 1) * width :],
                preferred_element_type=jnp.float32,
            ))

        @pl.when(kk > 0)
        def _():
            part = pl.multiple_of(row + (kk - 1) // 2 * half, half)
            column = pl.multiple_of(lax.rem(kk - 1, 2) * 2 * width, 2 * width)
            value = jnp.dot(
                tok_ref[pl.ds(part, half), :], w_ref[:, pl.ds(column, 2 * width)],
                preferred_element_type=jnp.float32,
            )
            put(slice(0, half), value[:, :width])
            put(slice(half, rows), value[:, width:])

    def pair_copy(kk, dest):
        return pltpu.make_async_remote_copy(
            pair_out.at[lax.rem(kk, 2), dest], pair_in.at[kk, dest], pair_ss.at[kk, dest], pair_rs.at[kk, dest],
            device_id=(g, partner), device_id_type=MESH,
        )

    def up_copy(kk, dest):
        return pltpu.make_async_remote_copy(
            pair_in.at[kk, dest], up_in.at[kk, dest], line_ss.at[kk, dest], up_rs.at[kk, dest],
            device_id=(g, lax.rem(s + 2, n)), device_id_type=MESH,
        )

    def dn_copy(kk, dest):
        return pltpu.make_async_remote_copy(
            pair_in.at[kk, dest], dn_in.at[kk, dest], line_ss.at[kk, dest], dn_rs.at[kk, dest],
            device_id=(g, lax.rem(s + n - 2, n)), device_id_type=MESH,
        )

    def kv_line(zz):
        block = kv_ref.at[2 * zz + c]
        return pltpu.make_async_remote_copy(
            block, block, kvl_ss.at[zz], kvl_rs.at[zz], device_id=(g, lax.rem(s + 2, n)), device_id_type=MESH
        )

    def kv_pair(zz):
        block = kv_ref.at[2 * zz + c]
        return pltpu.make_async_remote_copy(
            block, block, kvp_ss.at[zz], kvp_rs.at[zz], device_id=(g, partner), device_id_type=MESH
        )

    def kv_pair_wait(zz):
        block = kv_ref.at[2 * zz + 1 - c]
        return pltpu.make_async_remote_copy(
            block, block, kvp_ss.at[zz], kvp_rs.at[zz], device_id=(g, partner), device_id_type=MESH
        )

    def pair_stage(kk):
        @pl.loop(0, line)
        def _(i):
            dest = jnp.where(low, line - 1 - i, i)

            @pl.when(kk >= 2)
            def _():
                pair_copy(kk - 2, dest).wait_send()

            def put(part, value):
                pair_out[lax.rem(kk, 2), dest, part] = value.astype(jnp.bfloat16)

            product(kk, dest, 1 - c, put)
            pair_copy(kk, dest).start()

    def gathered(kk, dest):
        def put(part, value):
            total[part] = value

        product(kk, dest, c, put)
        pair_copy(kk, dest).wait_recv()
        total[...] += pair_in[kk, dest].astype(jnp.float32)

    def up_stage(kk):
        @pl.loop(0, line - 1 - z)
        def _(d):
            dest = line - 1 - d
            gathered(kk, dest)

            @pl.when(z > 0)
            def _():
                up_copy(kk, dest).wait_recv()
                total[...] += up_in[kk, dest].astype(jnp.float32)

            pair_in[kk, dest] = total[...].astype(jnp.bfloat16)
            up_copy(kk, dest).start()

    def dn_stage(kk):
        @pl.loop(0, z)
        def _(dest):
            gathered(kk, dest)

            @pl.when(z < line - 1)
            def _():
                dn_copy(kk, dest).wait_recv()
                total[...] += dn_in[kk, dest].astype(jnp.float32)

            pair_in[kk, dest] = total[...].astype(jnp.bfloat16)
            dn_copy(kk, dest).start()

    def wait_up_sends(kk):
        @pl.loop(0, line - 1 - z)
        def _(d):
            up_copy(kk, line - 1 - d).wait_send()

    def wait_dn_sends(kk):
        @pl.loop(0, z)
        def _(dest):
            dn_copy(kk, dest).wait_send()

    def rope(x, cosine, sine):
        return x * cosine + pltpu.roll(x, HEAD_DIM // 2, 1) * sine

    def finish(kk):
        gathered(kk, z)

        @pl.when(z > 0)
        def _():
            up_copy(kk, z).wait_recv()
            total[...] += up_in[kk, z].astype(jnp.float32)

        @pl.when(z < line - 1)
        def _():
            dn_copy(kk, z).wait_recv()
            total[...] += dn_in[kk, z].astype(jnp.float32)

        @pl.when(kk == 0)
        def _():
            value = total[...] + bias[:1, (chunks - 1) * width :]
            kv_ref[s, :, :HEAD_DIM] = rope(value[:, :HEAD_DIM], cos_ref[...], sin_ref[...]).astype(jnp.bfloat16)
            kv_ref[s, :, HEAD_DIM:] = value[:, HEAD_DIM:].astype(jnp.bfloat16)
            kv_pair(z).start()

            @pl.when(z < line - 1)
            def _():
                kv_line(z).start()

        @pl.when(kk > 0)
        def _():
            side = (kk - 1) // 2
            group = lax.rem(kk - 1, 2)
            mine = pl.ds(pl.multiple_of(side * half, half), half)
            for i in range(4):
                head = group * 4 + i
                lane = pl.multiple_of(head * HEAD_DIM, HEAD_DIM)
                value = total[(i // 2) * half : (i // 2 + 1) * half, (i % 2) * HEAD_DIM : (i % 2 + 1) * HEAD_DIM]
                value = rope(value + bias[:1, pl.ds(lane, HEAD_DIM)], cos_ref[mine, :], sin_ref[mine, :])
                queries[side, pl.ds(pl.multiple_of(head * half, half), half), :] = value.astype(jnp.bfloat16)

    def relay(h):
        @pl.when(h <= z)
        def _():
            zz = z - h
            kv_line(zz).wait_recv()

            @pl.when(z < line - 1)
            def _():
                kv_line(zz).start()

            kv_pair(zz).start()

    def attend(side):
        ahead = lax.broadcasted_iota(jnp.int32, (half, rows), 1) - lax.broadcasted_iota(jnp.int32, (half, rows), 0)
        ahead = ahead - side * half
        mine_ids = ids_col[pl.ds(pl.multiple_of(side * half, half), half), :1]
        ones = jnp.ones((rows, HEAD_DIM), jnp.bfloat16)
        scale = HEAD_DIM ** (-0.5)

        @pl.loop(0, GQA // 4)
        def _(quad):
            tops = [pl.multiple_of((2 * quad + i) * 2 * half, 2 * half) for i in range(2)]
            stacked = [queries[side, pl.ds(top, 2 * half), :] for top in tops]

            def step(j, state):
                keys = kv_ref[j, :, :HEAD_DIM]
                values = jnp.concatenate([kv_ref[j, :, HEAD_DIM:], ones], axis=1)
                allowed = (mine_ids == idall_ref[j, :1, :]) & (ahead <= (s - j) * rows)
                allowed = jnp.concatenate([allowed, allowed], axis=0)
                new = []
                for i in range(2):
                    row_max, weighted = state[i]
                    scores = lax.dot_general(
                        stacked[i], keys, (((1,), (1,)), ((), ())), preferred_element_type=jnp.float32
                    )
                    scores = jnp.where(allowed, scores * scale, neg_large)
                    new_max = jnp.maximum(row_max, jnp.max(scores, axis=1, keepdims=True))
                    exps = jnp.where(allowed, jnp.exp(scores - new_max), 0.0)
                    update = jnp.dot(exps.astype(jnp.bfloat16), values, preferred_element_type=jnp.float32)
                    new.append((new_max, weighted * jnp.exp(row_max - new_max) + update))
                return tuple(new)

            initial = (
                jnp.full((2 * half, 1), neg_large, jnp.float32),
                jnp.zeros((2 * half, 2 * HEAD_DIM), jnp.float32),
            )
            state = lax.fori_loop(0, s + 1, step, (initial, initial))
            for i in range(2):
                weighted = state[i][1]
                value = (weighted[:, :HEAD_DIM] / weighted[:, HEAD_DIM:]).astype(jnp.bfloat16)
                for part in range(2):
                    lane = pl.multiple_of((4 * quad + 2 * i + part) * HEAD_DIM, HEAD_DIM)
                    attended[side, :, pl.ds(lane, HEAD_DIM)] = value[part * half : (part + 1) * half]

    def mixed(side, pos, t):
        m = side * passes + pos * tiles + t
        w_copy(m).wait()
        value = jnp.dot(attended[side], weights[lax.rem(m, slots)], preferred_element_type=jnp.float32)

        @pl.when(m + slots < 2 * passes)
        def _():
            w_copy(m + slots).start()

        return value

    def copy1(side, slot, t):
        return pltpu.make_async_remote_copy(
            send1.at[side, slot, t], recv1.at[side, slot, t], ss1.at[side, slot, t], rs1.at[side, slot, t],
            device_id=(first_peer(t), s), device_id_type=MESH,
        )

    def copy2(side, t):
        return pltpu.make_async_remote_copy(
            send2.at[side, t], recv2.at[side, t], ss2.at[side, t], rs2.at[side, t],
            device_id=(second_peer(t), s), device_id_type=MESH,
        )

    def send_out(side):
        @pl.loop(0, 2 * tiles)
        def _(m):
            slot, t = m // tiles, lax.rem(m, tiles)
            send1[side, slot, t] = mixed(side, slot, t).astype(jnp.bfloat16)
            copy1(side, slot, t).start()

    def pass_on(side):
        @pl.loop(0, tiles)
        def _(t):
            kept[side, t] = mixed(side, 2, t)

        @pl.loop(0, tiles)
        def _(t):
            value = mixed(side, 3, t)
            copy1(side, 0, t).wait_recv()
            send2[side, t] = (value + recv1[side, 0, t].astype(jnp.float32)).astype(jnp.bfloat16)
            copy2(side, t).start()

    def collect(side):
        @pl.loop(0, tiles)
        def _(t):
            copy1(side, 1, t).wait_recv()
            copy2(side, t).wait_recv()
            value = kept[side, t] + recv1[side, 1, t].astype(jnp.float32) + recv2[side, t].astype(jnp.float32)
            mine = pl.ds(pl.multiple_of(side * half, half), half)
            out_ref[mine, pl.ds(pl.multiple_of(t * wide, wide), wide)] = value.astype(jnp.bfloat16)

    def primary(kk):
        @pl.when(low)
        def _():
            up_stage(kk)

        @pl.when(jnp.logical_not(low))
        def _():
            dn_stage(kk)

    def secondary(kk):
        @pl.when(low)
        def _():
            dn_stage(kk)

        @pl.when(jnp.logical_not(low))
        def _():
            up_stage(kk)

    def wait_primary(kk):
        @pl.when(low)
        def _():
            wait_up_sends(kk)

        @pl.when(jnp.logical_not(low))
        def _():
            wait_dn_sends(kk)

    def wait_secondary(kk):
        @pl.when(low)
        def _():
            wait_dn_sends(kk)

        @pl.when(jnp.logical_not(low))
        def _():
            wait_up_sends(kk)

    pair_stage(0)
    for i in range(1, n):
        id_copy(i).start()

    @pl.loop(0, chunks)
    def _(kk):
        @pl.when(kk >= 2)
        def _():
            wait_primary(kk - 2)

        primary(kk)

        @pl.when(kk == 0)
        def _():
            angles = (s * rows + lax.broadcasted_iota(jnp.int32, (rows, HEAD_DIM), 0)).astype(
                jnp.float32
            ) * freq_ref[...]
            lane = lax.broadcasted_iota(jnp.int32, (rows, HEAD_DIM), 1)
            sine = jnp.sin(angles)
            cos_ref[...] = jnp.cos(angles)
            sin_ref[...] = jnp.where(lane < HEAD_DIM // 2, -sine, sine)

        @pl.when(kk + 1 < chunks)
        def _():
            pair_stage(kk + 1)

        @pl.when(kk >= 1)
        def _():
            secondary(kk - 1)

        @pl.when(kk >= 2)
        def _():
            finish(kk - 2)

    for i in range(1, n):
        id_copy(i).wait_send()
        id_wait(i).wait_recv()

    @pl.loop(1, line)
    def _(h):
        relay(h)

    @pl.loop(0, z + 1)
    def _(zz):
        kv_pair_wait(zz).wait_recv()

    @pl.loop(0, 2)
    def _(side):
        attend(side)
        send_out(side)

        @pl.when(side == 0)
        def _():
            secondary(chunks - 1)
            finish(chunks - 2)

        pass_on(side)

        @pl.when(side == 0)
        def _():
            finish(chunks - 1)

    @pl.loop(0, 2)
    def _(side):
        collect(side)

    @pl.loop(0, chunks)
    def _(kk):
        @pl.when(kk >= chunks - 2)
        def _():
            wait_primary(kk)

            @pl.loop(0, line)
            def _(dest):
                pair_copy(kk, dest).wait_send()

        wait_secondary(kk)

    @pl.loop(0, z + 1)
    def _(zz):
        kv_pair(zz).wait_send()

        @pl.when(z < line - 1)
        def _():
            kv_line(zz).wait_send()

    @pl.loop(0, 2)
    def _(side):
        @pl.loop(0, tiles)
        def _(t):
            copy1(side, 0, t).wait_send()
            copy1(side, 1, t).wait_send()
            copy2(side, t).wait_send()


def body(seq, groups, tokens, proj_weight, proj_bias, out_weight, doc_ids):
    rows = doc_ids.shape[0]
    columns = proj_weight.shape[1]
    width = 2 * HEAD_DIM
    chunks = columns // width
    line = seq // 2
    half = rows // 2
    q_width = GQA * HEAD_DIM
    block = out_weight.shape[1] // groups
    wide = 4 * HEAD_DIM
    tiles = block // wide
    slots = 2 * tiles
    inverse_freq = theta_base ** (-(jnp.arange(HEAD_DIM // 2, dtype=jnp.float32) * 2.0) / HEAD_DIM)
    freq = jnp.concatenate([inverse_freq, inverse_freq])[None, :]
    vmem = pl.BlockSpec(memory_space=pltpu.VMEM)
    dma = pltpu.SemaphoreType.DMA
    bf16, f32, i32 = jnp.bfloat16, jnp.float32, jnp.int32

    return pl.pallas_call(
        functools.partial(layer_kernel, line, chunks, rows, width, groups, tiles, wide, slots),
        out_shape=jax.ShapeDtypeStruct((rows, block), bf16),
        in_specs=[vmem] * 5 + [pl.BlockSpec(memory_space=pl.ANY)],
        out_specs=vmem,
        scratch_shapes=[
            pltpu.VMEM((2, line, rows, width), bf16),
            pltpu.VMEM((chunks, line, rows, width), bf16),
            pltpu.VMEM((chunks, line, rows, width), bf16),
            pltpu.VMEM((chunks, line, rows, width), bf16),
            pltpu.VMEM((rows, width), f32),
            pltpu.VMEM((2, GQA * half, HEAD_DIM), bf16),
            pltpu.VMEM((seq, rows, width), bf16),
            pltpu.VMEM((2, half, q_width), bf16),
            pltpu.VMEM((8, rows), i32),
            pltpu.VMEM((rows, HEAD_DIM), i32),
            pltpu.VMEM((seq, 8, rows), i32),
            pltpu.VMEM((8, columns), f32),
            pltpu.VMEM((rows, HEAD_DIM), f32),
            pltpu.VMEM((rows, HEAD_DIM), f32),
            pltpu.VMEM((slots, q_width, wide), bf16),
            pltpu.VMEM((2, tiles, half, wide), f32),
            pltpu.VMEM((2, 2, tiles, half, wide), bf16),
            pltpu.VMEM((2, 2, tiles, half, wide), bf16),
            pltpu.VMEM((2, tiles, half, wide), bf16),
            pltpu.VMEM((2, tiles, half, wide), bf16),
        ]
        + [dma((chunks, line))] * 5
        + [dma((seq,))] * 2
        + [dma((line,))] * 4
        + [dma((slots,)), dma((2, 2, tiles)), dma((2, 2, tiles)), dma((2, tiles)), dma((2, tiles))],
        compiler_params=pltpu.CompilerParams(
            collective_id=0, has_side_effects=True, vmem_limit_bytes=67043328
        ),
        name="layer",
    )(tokens, proj_weight, proj_bias[None, :], freq, doc_ids[None, :], out_weight)


def solution(mesh):
    return jax.shard_map(
        functools.partial(body, mesh.shape["seq"], mesh.shape["grp"]),
        mesh=mesh,
        in_specs=(P(None, "seq"), P("seq", "grp"), P("grp"), P("grp", None), P("seq")),
        out_specs=P("seq", "grp"),
        check_vma=False,
    )
```

time: 284 us -> 116 us (0.41)
  waiting for transfers between devices: 184 us -> 0 us
  Pallas kernels: 0 us -> 111 us
  blocking collectives: 38.6 us -> 0 us
  matrix products: 29.8 us -> 0 us
  between operations: 14.2 us -> 0.01 us
  other arithmetic: 11.2 us -> 0.68 us
    reduce_scatter x2 -> x0, waiting for transfers between devices: 183 us -> none  [the longest x1 96.7 us: body(): lax.psum_scatter(jnp.dot(tokens, proj_weight, preferred_element_type=jnp....]
    pallas_call x0 -> x1, Pallas kernels: none -> 111 us  [body(): pl.pallas_call(functools.partial(layer_kernel, line, chunks, rows, width,...]
    all_gather x3 -> x0, blocking collectives: 38.6 us -> none  [the longest x1 15.6 us: body(): key_block = lax.all_gather(key_rows, 'seq', axis=0, tiled=True)]
    dot_general x4 -> x0, matrix products: 29.8 us -> none  [the longest x1 12.9 us: body(): jnp.dot(attended, out_weight, preferred_element_type=jnp.float32)]
    reduce_sum x1 -> x0, other arithmetic: 4.03 us -> none  [compute(): new_sum = jnp.sum(weights, axis=-1)]
    convert_element_type x6 -> x0, other arithmetic: 3.06 us -> none  [the longest x1 2.71 us: body(): lax.psum_scatter(partial_value, 'grp', scatter_dimension=1, tiled=True)]
  transfers between devices with their start and end apart: 2 -> 0, of which waited for: 2 -> 0; matrix products, arithmetic and copies ran while one was open for 1% -> 0% of each run, Pallas kernels for 0% -> 0%
where the time goes in v2:
time: 116 us
  Pallas kernels  111 us (96%)
  local copies, waits for them, and re-layouts  3.59 us (3%)
    pallas_call x1, Pallas kernels, body(): pl.pallas_call(functools.partial(layer_kernel, line, chunks, rows, width,...  111 us

profile of v2, /device:TPU:25, one launch (start us, length us, event | category | flops | bytes accessed | tf_op | source)
XLA Modules:
  0.0 115.6 jit_solution(9689968432598841718)
XLA Ops:
  0.0 0.7 maximum_bitcast_fusion.freq_ref
  0.7 1.3 %broadcast_in_dim.9.bias_ref = bf16[1,1280]{1,0:T(2,128)(2,1)} reshape(bf16[1280]{0:T(1024)(128)(2,1)} %param.7) | data formatting | bytes 5120 | tf_op jit(solution)/shard_map/broadcast_in_dim | solution.py:528
  2.0 111.3 %layer.1 = bf16[256,2048]{1,0:T(8,128)(2,1)} custom-call(bf16[2048,1024]{1,0:T(8,128)(2,1)} %tok_ref.1, bf16[1024,1280]{1,0:T(8,128)(2,1)} %w_ref.1, bf16[1,1280]{1,0:T(2,128)(2,1)} %broadcast_in_dim.9.bias_ref, f32[1,128]{1,0:T(1,128)} %maximum_bitcast_fusion.freq_ref, s32[1,256]{1,0:T(1,128)} %bitcast.3, bf16[1024,8192]{1,0:T(8,128)(2,1)} %ow_ref.1), custom_call_target="tpu_custom_call" | custom-call | tf_op jit(solution)/shard_map/layer/pallas_call | solution.py:493
  113.3 2.3 %copy.7 = bf16[256,2048]{1,0:T(8,128)(2,1)} copy(bf16[256,2048]{1,0:T(8,128)(2,1)} %layer.1) | data formatting | bytes 2097152
  (1 shorter events, 0.0 us)

commit v3 on v2

--- a/solution.py
+++ b/solution.py
@@ -13,6 +13,7 @@
 
 theta_base = 1000000.0
 neg_large = -1e30
+log2_e = 1.4426950408889634
 
 
 def layer_kernel(
@@ -253,7 +254,7 @@
         ahead = ahead - side * half
         mine_ids = ids_col[pl.ds(pl.multiple_of(side * half, half), half), :1]
         ones = jnp.ones((rows, HEAD_DIM), jnp.bfloat16)
-        scale = HEAD_DIM ** (-0.5)
+        scale = HEAD_DIM ** (-0.5) * log2_e
 
         @pl.loop(0, GQA // 4)
         def _(quad):
@@ -273,9 +274,9 @@
                     )
                     scores = jnp.where(allowed, scores * scale, neg_large)
                     new_max = jnp.maximum(row_max, jnp.max(scores, axis=1, keepdims=True))
-                    exps = jnp.where(allowed, jnp.exp(scores - new_max), 0.0)
+                    exps = jnp.exp2(scores - new_max)
                     update = jnp.dot(exps.astype(jnp.bfloat16), values, preferred_element_type=jnp.float32)
-                    new.append((new_max, weighted * jnp.exp(row_max - new_max) + update))
+                    new.append((new_max, weighted * jnp.exp2(row_max - new_max) + update))
                 return tuple(new)
 
             initial = (
@@ -389,7 +390,15 @@
 
         primary(kk)
 
-        @pl.when(kk == 0)
+        @pl.when(kk + 1 < chunks)
+        def _():
+            pair_stage(kk + 1)
+
+        @pl.when(kk >= 1)
+        def _():
+            secondary(kk - 1)
+
+        @pl.when(kk == 1)
         def _():
             angles = (s * rows + lax.broadcasted_iota(jnp.int32, (rows, HEAD_DIM), 0)).astype(
                 jnp.float32
@@ -398,14 +407,6 @@
             sine = jnp.sin(angles)
             cos_ref[...] = jnp.cos(angles)
             sin_ref[...] = jnp.where(lane < HEAD_DIM // 2, -sine, sine)
-
-        @pl.when(kk + 1 < chunks)
-        def _():
-            pair_stage(kk + 1)
-
-        @pl.when(kk >= 1)
-        def _():
-            secondary(kk - 1)
 
         @pl.when(kk >= 2)
         def _():

time: 116 us -> 116 us (level)
  no operation moved by 1% of the time
where the time goes in v3:
time: 116 us
  Pallas kernels  111 us (96%)
  local copies, waits for them, and re-layouts  3.59 us (3%)
    pallas_call x1, Pallas kernels, body(): pl.pallas_call(functools.partial(layer_kernel, line, chunks, rows, width,...  111 us

profile of v3, /device:TPU:25, one launch (start us, length us, event | category | flops | bytes accessed | tf_op | source)
XLA Modules:
  0.0 115.6 jit_solution(12669828141544647040)
XLA Ops:
  0.0 0.7 maximum_bitcast_fusion.freq_ref
  0.7 1.3 %broadcast_in_dim.9.bias_ref = bf16[1,1280]{1,0:T(2,128)(2,1)} reshape(bf16[1280]{0:T(1024)(128)(2,1)} %param.7) | data formatting | bytes 5120 | tf_op jit(solution)/shard_map/broadcast_in_dim | solution.py:529
  2.0 111.3 %layer.1 = bf16[256,2048]{1,0:T(8,128)(2,1)} custom-call(bf16[2048,1024]{1,0:T(8,128)(2,1)} %tok_ref.1, bf16[1024,1280]{1,0:T(8,128)(2,1)} %w_ref.1, bf16[1,1280]{1,0:T(2,128)(2,1)} %broadcast_in_dim.9.bias_ref, f32[1,128]{1,0:T(1,128)} %maximum_bitcast_fusion.freq_ref, s32[1,256]{1,0:T(1,128)} %bitcast.3, bf16[1024,8192]{1,0:T(8,128)(2,1)} %ow_ref.1), custom_call_target="tpu_custom_call" | custom-call | tf_op jit(solution)/shard_map/layer/pallas_call | solution.py:494
  113.3 2.3 %copy.7 = bf16[256,2048]{1,0:T(8,128)(2,1)} copy(bf16[256,2048]{1,0:T(8,128)(2,1)} %layer.1) | data formatting | bytes 2097152
  (1 shorter events, 0.0 us)
